TPU v7x, 32 devices: a whole 2x2x4 slice. The times are simulated.
32 devices in a mesh: dp: 4 (over y, x), vocab: 8 (over z, core).
Axes of the slice: x: 2, y: 2, z: 4, core: 2. Of those that a mesh axis runs over, the one named last changes fastest.
Arguments:
- hidden: bfloat16 [512, 8192], P('dp', 'vocab'), may hold values from -20 to 20
- weight: bfloat16 [8192, 4752], P('dp', 'vocab'), may hold values from -0.198873782 to 0.198873782
- targets: int32 [512], P('dp'), may hold values from 0 to 4751
- loss_mask: int32 [512], P('dp'), may hold values 0 or 1
Outputs:
- grad_hidden: bfloat16 [512, 8192], P('dp', 'vocab')
- grad_weight: bfloat16 [8192, 4752], P('dp', 'vocab')
- token_loss: float32 [512], P('dp')
- grad_norm: float32 [], replicated
All inputs are finite; a program needn't handle non-finite values. No bound on the sum of `loss_mask` on one device may be relied on, other than what follows from the above.
Results may differ from a plain program's by a relative error of at most 0.0034.
Values may be sent and summed in bfloat16 or wider, within the bound.
A program may use at most 128 MiB of HBM per device.

v0:
```python
import jax
import jax.numpy as jnp
from jax import lax
from jax.sharding import PartitionSpec as P

loss_scale = 16.0


def on_device(hidden, weight, targets, loss_mask):
    shard_width = weight.shape[1]
    col_offset = lax.axis_index("vocab") * shard_width
    full_hidden = lax.all_gather(hidden, "vocab", axis=1, tiled=True)
    hidden_block = lax.all_to_all(full_hidden, "dp", split_axis=1, concat_axis=0, tiled=True)
    full_weight = lax.all_gather(weight, "dp", axis=0, tiled=True)
    logits = jnp.dot(full_hidden, full_weight, preferred_element_type=jnp.float32)
    row_targets, row_mask = (targets, loss_mask)
    local_col = row_targets - col_offset
    onehot = (lax.broadcasted_iota(jnp.int32, logits.shape, 1) == local_col[:, None]).astype(
        jnp.float32
    )
    target_local = jnp.sum(logits * onehot, axis=1)
    local_top = jnp.max(logits, axis=1)
    row_top = lax.pmax(local_top, "vocab")
    local_sum = jnp.sum(jnp.exp(logits - row_top[:, None]), axis=1)
    exp_sum, target_logit = lax.psum((local_sum, target_local), "vocab")
    log_total = row_top + jnp.log(exp_sum)
    row_keep = row_mask.astype(jnp.float32)
    loss_rows = row_keep * (log_total - target_logit)
    softmax = jnp.exp(logits - log_total[:, None])
    dlogits = (loss_scale * row_keep[:, None] * (softmax - onehot)).astype(jnp.bfloat16)
    dlog_all = lax.all_gather(dlogits, "dp", axis=0, tiled=True)
    hidden_terms = lax.dot_general(
        dlogits, full_weight, (((1,), (1,)), ((), ())), preferred_element_type=jnp.float32
    )
    hidden_grad_full = lax.psum_scatter(hidden_terms, "vocab", scatter_dimension=1, tiled=True)
    weight_grad_full = lax.dot_general(
        hidden_block, dlog_all, (((0,), (0,)), ((), ())), preferred_element_type=jnp.float32
    )
    local_squares = jnp.sum(weight_grad_full * weight_grad_full) + jnp.sum(
        hidden_grad_full * hidden_grad_full
    )
    squares_total = lax.psum(local_squares, ("dp", "vocab"))
    return (
        hidden_grad_full.astype(jnp.bfloat16),
        weight_grad_full.astype(jnp.bfloat16),
        loss_rows,
        jnp.sqrt(squares_total),
    )


def solution(mesh):
    placed = (P("dp", "vocab"), P("dp", "vocab"), P("dp"), P("dp"))
    return jax.shard_map(
        on_device,
        mesh=mesh,
        in_specs=placed,
        out_specs=(P("dp", "vocab"), P("dp", "vocab"), P("dp"), P()),
        check_vma=False,
    )
```

profile of v0, /device:TPU:12, one launch (start us, length us, event | category | flops | bytes accessed | tf_op | source)
XLA Modules:
  0.0 285.6 jit_solution(2477782353101069427)
XLA Ops:
  7.2 0.0 copy-start.2
  7.2 0.0 all-gather.3.cloned.1.call-start
  7.2 1.8 copy.8
  9.0 0.0 all-gather.3.cloned.1.call-update
  9.0 0.0 all-gather.5.cloned.1.call-start
  9.1 0.7 all-gather.5.cloned.1.call-update
  9.8 0.0 reduce-scatter.2.cloned.1.call-start
  9.8 0.0 copy-done.2
  9.9 0.0 copy-start.1
  9.9 30.6 %all-gather.3.cloned.1.call-done = bf16[128,8192]{0,1:T(8,128)(2,1)} async-done(((bf16[128,1024]{0,1:T(8,128)(2,1)}), bf16[128,8192]{0,1:T(8,128)(2,1)}) %all-gather.3.cloned.1.call-update) | async-done | bytes 2097168 | tf_op jit(solution)/shard_map/all_gather | solution.py:12
  40.4 100.8 %all-gather.5.cloned.1.call-done = bf16[8192,594]{0,1:T(8,128)(2,1)} async-done(((bf16[2048,594]{0,1:T(8,128)(2,1)}), bf16[8192,594]{0,1:T(8,128)(2,1)}) %all-gather.5.cloned.1.call-update) | async-done | bytes 9732112 | tf_op jit(solution)/shard_map/all_gather | solution.py:14
  141.2 6.2 %fusion = (f32[128]{0:T(128)S(1)}, f32[128,594]{0,1:T(8,128)S(1)}) fusion(bf16[128,8192]{0,1:T(8,128)(2,1)} %all-gather.3.cloned.1.call-done, bf16[8192,594]{0,1:T(8,128)(2,1)} %all-gather.5.cloned.1.call-done), kind=kOutput, calls=%fused_computation.11 | convolution fusion | flops 1245784192 | bytes 12133888 | tf_op jit(solution)/shard_map/dot_general | solution.py:15
  147.4 12.7 %pmax.7 = f32[128]{0:T(128)S(1)} all-reduce(f32[128]{0:T(128)S(1)} %get-tuple-element.15), channel_id=1, replica_groups=mesh['dp'=4,'vocab'=8] {'vocab'}, use_global_device_ids=true, to_apply=%region_1.0 | all-reduce | flops 128 | bytes 1024 | tf_op jit(solution)/shard_map/pmax | solution.py:23
  160.1 0.1 select_reduce_fusion
  160.2 13.6 %all-reduce = (f32[128]{0:T(128)S(1)}, f32[128]{0:T(128)S(1)}) all-reduce(f32[128]{0:T(128)S(1)} %get-tuple-element.5, f32[128]{0:T(128)S(1)} %get-tuple-element.4), channel_id=1, replica_groups=mesh['dp'=4,'vocab'=8] {'vocab'}, use_global_device_ids=true, to_apply=%region_3.0 | all-reduce | flops 256 | bytes 2048 | tf_op jit(solution)/shard_map/psum | solution.py:25
  173.8 0.0 copy-done.1
  173.8 0.5 subtract_multiply_fusion
  174.3 0.1 multiply_convert_fusion
  174.4 8.0 %fusion.1 = f32[128,8192]{1,0:T(8,128)} fusion(bf16[128,594]{0,1:T(8,128)(2,1)S(1)} %multiply_convert_fusion, bf16[8192,594]{0,1:T(8,128)(2,1)} %all-gather.5.cloned.1.call-done), kind=kOutput, calls=%fused_computation.12 | convolution fusion | flops 1245708288 | bytes 14078464 | tf_op jit(solution)/shard_map/dot_general | solution.py:32
  182.4 0.0 copy-start
  182.4 0.0 reduce-scatter.2.cloned.1.call-update
  182.4 1.6 copy-done
  184.0 28.4 %all_to_all.19 = bf16[128,4,2048]{0,2,1:T(8,128)(2,1)} all-to-all(bf16[128,4,2048]{0,2,1:T(8,128)(2,1)S(1)} %bitcast.11), channel_id=1, replica_groups=mesh['dp'=4,'vocab'=8] {'dp'}, dimensions={1} | all-to-all | bytes 4194304 | tf_op jit(solution)/shard_map/all_to_all | solution.py:13
  212.3 2.9 %copy.9 = bf16[4,128,2048]{2,1,0:T(8,128)(2,1)S(1)} copy(bf16[4,128,2048]{1,2,0:T(8,128)(2,1)} %bitcast.12) | data formatting | bytes 4194304 | tf_op jit(solution)/shard_map/all_to_all | solution.py:13
  215.3 10.0 %all_gather.11 = bf16[512,594]{0,1:T(8,128)(2,1)S(1)} all-gather(bf16[128,594]{0,1:T(8,128)(2,1)S(1)} %multiply_convert_fusion), channel_id=1, replica_groups=mesh['dp'=4,'vocab'=8] {'dp'}, dimensions={0}, use_global_device_ids=true | all-gather | bytes 760320 | tf_op jit(solution)/shard_map/all_gather | solution.py:31
  225.3 3.6 %multiply_reduce_fusion = (f32[]{:T(128)}, bf16[2048,594]{0,1:T(8,128)(2,1)}) fusion(bf16[512,594]{0,1:T(8,128)(2,1)S(1)} %all_gather.11, bf16[512,2048]{1,0:T(8,128)(2,1)S(1)} %bitcast.13), kind=kOutput, calls=%fused_computation | convolution fusion | flops 1249357824 | bytes 5138436 | tf_op jit(solution)/shard_map/dot_general | solution.py:36
  228.9 1.2 reduce-scatter.2.cloned.1.call-done
  230.1 2.6 multiply_reduce_fusion.1
  234.0 43.3 %psum.23 = f32[]{:T(128)} all-reduce(f32[]{:T(128)S(6)} %add.15), channel_id=1, replica_groups=mesh['dp'=4,'vocab'=8] {'dp','vocab'}, use_global_device_ids=true, to_apply=%region_9.0 | all-reduce | flops 1 | bytes 8 | tf_op jit(solution)/shard_map/psum | solution.py:42
  (1 shorter events, 0.0 us)
Async XLA Ops:
  7.2 2.7 copy-start.2
  7.2 33.3 %all-gather.3.cloned.1.call-start = ((), (), s32[]{:S(2)}) async-start(), calls=%async_computation.2 | async-start | bytes 2359296 | tf_op jit(solution)/shard_map/all_gather | solution.py:12
  9.0 132.2 %all-gather.5.cloned.1.call-start = ((), (), s32[]{:S(2)}) async-start(), calls=%async_computation.3 | async-start | bytes 12288000 | tf_op jit(solution)/shard_map/all_gather | solution.py:14
  9.8 220.3 %reduce-scatter.2.cloned.1.call-start = ((), (), s32[]{:S(2)}) async-start(), calls=%async_computation.4 | async-start | bytes 4718592 | tf_op jit(solution)/shard_map/reduce_scatter | solution.py:35
  9.9 163.9 %copy-start.1 = (s32[128]{0:T(128)S(1)}, s32[128]{0:T(128)}, u32[]{:S(2)}) copy-start(s32[128]{0:T(128)} %param.7) | copy-start | bytes 1540
  182.4 1.6 copy-start
Sparse Core Ops, SparseCore 0:
  10.2 30.2 all-gather.2
  42.3 98.8 all-gather.4
  182.5 47.5 reduce-scatter.1
where the time goes:
time: 286 us
  waiting for transfers between devices  133 us (47%)
  blocking collectives  108 us (38%)
  matrix products  17.8 us (6%)
  between operations  17 us (6%)
  local copies, waits for them, and re-layouts  6.31 us (2%)
  other arithmetic  3.29 us (1%)
    all_gather x1, waiting for transfers between devices, on_device(): full_weight = lax.all_gather(weight, 'dp', axis=0, tiled=True)  101 us
    psum x1, blocking collectives, on_device(): squares_total = lax.psum(local_squares, ('dp', 'vocab'))  43.3 us
    all_gather x1, waiting for transfers between devices, on_device(): full_hidden = lax.all_gather(hidden, 'vocab', axis=1, tiled=True)  30.6 us
    all_to_all x1, blocking collectives, on_device(): lax.all_to_all(full_hidden, 'dp', split_axis=1, concat_axis=0, tiled=True)  28.4 us
    psum x1, blocking collectives, on_device(): exp_sum, target_logit = lax.psum((local_sum, target_local), 'vocab')  13.6 us
    pmax x1, blocking collectives, on_device(): row_top = lax.pmax(local_top, 'vocab')  12.7 us
    all_gather x1, blocking collectives, on_device(): dlog_all = lax.all_gather(dlogits, 'dp', axis=0, tiled=True)  10 us
    dot_general x1, matrix products, on_device(): lax.dot_general(dlogits, full_weight, (((1,), (1,)), ((), ())), preferred...  8.01 us
  transfers between devices with their start and end apart: 3, of which 3 were waited for; matrix products, arithmetic and copies ran while one was open for 2% of the time, Pallas kernels for 0%

commit v1 on v0

--- a/solution.py
+++ b/solution.py
@@ -9,7 +9,8 @@
 def on_device(hidden, weight, targets, loss_mask):
     shard_width = weight.shape[1]
     col_offset = lax.axis_index("vocab") * shard_width
-    full_hidden = lax.all_gather(hidden, "vocab", axis=1, tiled=True)
+    blocks = lax.all_gather(hidden, "vocab")
+    full_hidden = jnp.concatenate(blocks, axis=1)
     hidden_block = lax.all_to_all(full_hidden, "dp", split_axis=1, concat_axis=0, tiled=True)
     full_weight = lax.all_gather(weight, "dp", axis=0, tiled=True)
     logits = jnp.dot(full_hidden, full_weight, preferred_element_type=jnp.float32)

time: 286 us -> 285 us (level)
    unnamed x7 -> x4, local copies, waits for them, and re-layouts: 3.37 us -> 0.01 us
    all_gather x1, waiting for transfers between devices: 101 us -> 97.7 us  [on_device(): full_weight = lax.all_gather(weight, 'dp', axis=0, tiled=True)]
    reshape x0 -> x1, local copies, waits for them, and re-layouts: none -> 3.03 us  [on_device(): full_hidden = jnp.concatenate(blocks, axis=1)]
  transfers between devices with their start and end apart: 3 -> 3, of which waited for: 3 -> 3; matrix products, arithmetic and copies ran while one was open for 2% -> 3% of each run, Pallas kernels for 0% -> 0%
where the time goes in v1:
time: 285 us; the launch traced here: 284 us
  waiting for transfers between devices  133 us (47%)
  blocking collectives  108 us (38%)
  matrix products  17.1 us (6%)
  between operations  17 us (6%)
  local copies, waits for them, and re-layouts  5.97 us (2%)
  other arithmetic  3.29 us (1%)
    all_gather x1, waiting for transfers between devices, on_device(): full_weight = lax.all_gather(weight, 'dp', axis=0, tiled=True)  97.7 us
    psum x1, blocking collectives, on_device(): squares_total = lax.psum(local_squares, ('dp', 'vocab'))  43.3 us
    all_gather x1, waiting for transfers between devices, on_device(): blocks = lax.all_gather(hidden, 'vocab')  31.1 us
    all_to_all x1, blocking collectives, on_device(): lax.all_to_all(full_hidden, 'dp', split_axis=1, concat_axis=0, tiled=True)  28.4 us
    psum x1, blocking collectives, on_device(): exp_sum, target_logit = lax.psum((local_sum, target_local), 'vocab')  13.6 us
    pmax x1, blocking collectives, on_device(): row_top = lax.pmax(local_top, 'vocab')  12.7 us
    all_gather x1, blocking collectives, on_device(): dlog_all = lax.all_gather(dlogits, 'dp', axis=0, tiled=True)  10 us
    dot_general x1, matrix products, on_device(): lax.dot_general(dlogits, full_weight, (((1,), (1,)), ((), ())), preferred...  8.01 us
  transfers between devices with their start and end apart: 3, of which 3 were waited for; matrix products, arithmetic and copies ran while one was open for 3% of the time, Pallas kernels for 0%

profile of v1, /device:TPU:12, one launch (start us, length us, event | category | flops | bytes accessed | tf_op | source)
XLA Modules:
  0.0 284.4 jit_solution(13133676767480511672)
XLA Ops:
  7.2 0.0 copy-start.1
  7.2 0.0 all-gather.6.cloned.1.call-start
  7.2 0.7 all-gather.6.cloned.1.call-update
  7.9 0.0 all-gather.4.cloned.1.call-start
  8.0 0.7 all-gather.4.cloned.1.call-update
  8.7 0.0 reduce-scatter.2.cloned.1.call-start
  8.7 0.0 copy-done.1
  8.7 31.1 %all-gather.6.cloned.1.call-done = bf16[1024,1024]{1,0:T(8,128)(2,1)} async-done(((bf16[128,1024]{1,0:T(8,128)(2,1)}), bf16[1024,1024]{1,0:T(8,128)(2,1)}) %all-gather.6.cloned.1.call-update) | async-done | bytes 2097168 | tf_op jit(solution)/shard_map/all_gather | solution.py:12
  39.9 3.0 %copy.9 = bf16[128,8,1024]{0,2,1:T(8,128)(2,1)S(1)} copy(bf16[128,8,1024]{2,0,1:T(8,128)(2,1)} %bitcast.18) | data formatting | bytes 4194304 | tf_op jit(solution)/shard_map/reshape | solution.py:13
  42.9 97.7 %all-gather.4.cloned.1.call-done = bf16[8192,594]{0,1:T(8,128)(2,1)} async-done(((bf16[2048,594]{0,1:T(8,128)(2,1)}), bf16[8192,594]{0,1:T(8,128)(2,1)}) %all-gather.4.cloned.1.call-update) | async-done | bytes 9732112 | tf_op jit(solution)/shard_map/all_gather | solution.py:15
  140.6 0.0 copy-start
  140.6 5.5 %fusion = (f32[128]{0:T(128)S(1)}, f32[128,594]{0,1:T(8,128)S(1)}) fusion(bf16[128,8192]{0,1:T(8,128)(2,1)S(1)} %bitcast.15, bf16[8192,594]{0,1:T(8,128)(2,1)} %all-gather.4.cloned.1.call-done), kind=kOutput, calls=%fused_computation.11 | convolution fusion | flops 1245784192 | bytes 12133888 | tf_op jit(solution)/shard_map/dot_general | solution.py:16
  146.1 12.7 %pmax.7 = f32[128]{0:T(128)S(1)} all-reduce(f32[128]{0:T(128)S(1)} %get-tuple-element.15), channel_id=1, replica_groups=mesh['dp'=4,'vocab'=8] {'vocab'}, use_global_device_ids=true, to_apply=%region_1.0 | all-reduce | flops 128 | bytes 1024 | tf_op jit(solution)/shard_map/pmax | solution.py:24
  158.8 0.1 select_reduce_fusion
  158.9 13.6 %all-reduce = (f32[128]{0:T(128)S(1)}, f32[128]{0:T(128)S(1)}) all-reduce(f32[128]{0:T(128)S(1)} %get-tuple-element.5, f32[128]{0:T(128)S(1)} %get-tuple-element.4), channel_id=1, replica_groups=mesh['dp'=4,'vocab'=8] {'vocab'}, use_global_device_ids=true, to_apply=%region_3.0 | all-reduce | flops 256 | bytes 2048 | tf_op jit(solution)/shard_map/psum | solution.py:26
  172.5 0.0 copy-done
  172.5 0.5 subtract_multiply_fusion
  173.0 0.1 multiply_convert_fusion
  173.1 8.0 %fusion.1 = f32[128,8192]{1,0:T(8,128)} fusion(bf16[128,594]{0,1:T(8,128)(2,1)S(1)} %multiply_convert_fusion, bf16[8192,594]{0,1:T(8,128)(2,1)} %all-gather.4.cloned.1.call-done), kind=kOutput, calls=%fused_computation.12 | convolution fusion | flops 1245708288 | bytes 14078464 | tf_op jit(solution)/shard_map/dot_general | solution.py:33
  181.1 0.0 reduce-scatter.2.cloned.1.call-update
  181.2 28.4 %all_to_all.19 = bf16[128,4,2048]{0,2,1:T(8,128)(2,1)} all-to-all(bf16[128,4,2048]{0,2,1:T(8,128)(2,1)S(1)} %bitcast.16), channel_id=1, replica_groups=mesh['dp'=4,'vocab'=8] {'dp'}, dimensions={1} | all-to-all | bytes 4194304 | tf_op jit(solution)/shard_map/all_to_all | solution.py:14
  209.5 2.9 %copy.11 = bf16[4,128,2048]{2,1,0:T(8,128)(2,1)S(1)} copy(bf16[4,128,2048]{1,2,0:T(8,128)(2,1)} %bitcast.17) | data formatting | bytes 4194304 | tf_op jit(solution)/shard_map/all_to_all | solution.py:14
  212.5 10.0 %all_gather.15 = bf16[512,594]{0,1:T(8,128)(2,1)S(1)} all-gather(bf16[128,594]{0,1:T(8,128)(2,1)S(1)} %multiply_convert_fusion), channel_id=1, replica_groups=mesh['dp'=4,'vocab'=8] {'dp'}, dimensions={0}, use_global_device_ids=true | all-gather | bytes 760320 | tf_op jit(solution)/shard_map/all_gather | solution.py:32
  222.5 3.6 %multiply_reduce_fusion = (f32[]{:T(128)}, bf16[2048,594]{0,1:T(8,128)(2,1)}) fusion(bf16[512,594]{0,1:T(8,128)(2,1)S(1)} %all_gather.15, bf16[512,2048]{1,0:T(8,128)(2,1)S(1)} %bitcast.19), kind=kOutput, calls=%fused_computation | convolution fusion | flops 1249357824 | bytes 5138436 | tf_op jit(solution)/shard_map/dot_general | solution.py:37
  226.1 2.8 reduce-scatter.2.cloned.1.call-done
  228.9 2.6 multiply_reduce_fusion.1
  232.8 43.3 %psum.23 = f32[]{:T(128)} all-reduce(f32[]{:T(128)S(6)} %add.15), channel_id=1, replica_groups=mesh['dp'=4,'vocab'=8] {'dp','vocab'}, use_global_device_ids=true, to_apply=%region_9.0 | all-reduce | flops 1 | bytes 8 | tf_op jit(solution)/shard_map/psum | solution.py:43
  (1 shorter events, 0.0 us)
Async XLA Ops:
  7.2 1.5 copy-start.1
  7.2 32.7 %all-gather.6.cloned.1.call-start = ((), (), s32[]{:S(2)}) async-start(), calls=%async_computation.4 | async-start | bytes 2359296 | tf_op jit(solution)/shard_map/all_gather | solution.py:12
  7.9 132.7 %all-gather.4.cloned.1.call-start = ((), (), s32[]{:S(2)}) async-start(), calls=%async_computation.2 | async-start | bytes 12288000 | tf_op jit(solution)/shard_map/all_gather | solution.py:15
  8.7 220.2 %reduce-scatter.2.cloned.1.call-start = ((), (), s32[]{:S(2)}) async-start(), calls=%async_computation.3 | async-start | bytes 4718592 | tf_op jit(solution)/shard_map/reduce_scatter | solution.py:36
  140.6 31.9 %copy-start = (s32[128]{0:T(128)S(1)}, s32[128]{0:T(128)}, u32[]{:S(2)}) copy-start(s32[128]{0:T(128)} %param.7) | copy-start | bytes 1540
Sparse Core Ops, SparseCore 0:
  9.6 30.2 all-gather.5
  41.7 98.8 all-gather.3
  181.3 47.5 reduce-scatter.1
